TPU v7x, 256 devices: a whole 4x4x8 slice. The times are simulated.
256 devices in a mesh: row: 8 (over x, core), col: 32 (over y, z).
Axes of the slice: x: 4, y: 4, z: 8, core: 2. Of those that a mesh axis runs over, the one named last changes fastest.
Arguments:
- tensor: float32 [1024, 64, 4096], P(None, 'row', 'col'), may hold values from -60 to 60, as said below
- factor_two: float32 [64, 32], P('row'), may hold values from -0.75 to 0.75
- factor_three: float32 [128, 32], P('col'), may hold values from -0.5 to 0.5
- factor_four: float32 [32, 16], replicated, may hold values from -1 to 1
- factor_init: float32 [1024, 64], replicated, may hold values from -6 to 6
Outputs:
- factor_new: float32 [1024, 64], replicated
- core: float32 [64, 32, 32, 16], P(None, 'row', 'col')
Inputs may be any that keep to these rules, and one draw needn't show every extreme that they name: `tensor`: scales vary from slab to slab.
All inputs are finite; a program needn't handle non-finite values.
Results may differ from a plain program's by a relative error of at most 0.00013.
Values sent between devices are 32-bit elements; how exact they have to be, the bound alone decides.
No kernel may reach another device: no remote copies, remote signals or barrier semaphores. Data moves between devices by JAX's collectives and lax.ppermute only.
A program may use at most 128 MiB of HBM per device.

v0:
```python
import jax
import jax.numpy as jnp
from jax import lax
from jax.sharding import Mesh
from jax.sharding import PartitionSpec as P

ROW = ("row_0", "row_1")
COL = ("col_0", "col_1")


def from_everyone(array, axis):
    copies = jnp.broadcast_to(array, (lax.axis_size(axis), *array.shape))
    return lax.all_to_all(copies, axis, split_axis=0, concat_axis=0, tiled=True)


def joined_along(tiles, dim):
    shape = list(tiles.shape[1:])
    shape[dim] *= tiles.shape[0]
    return jnp.moveaxis(tiles, 0, dim).reshape(shape)


def gathered_copies(array, axis, dim):
    tiles = from_everyone(array, axis)
    return joined_along(tiles, dim)


def split_up(array, dim, length):
    shape = array.shape
    tiles = array.reshape(*shape[:dim], length, shape[dim] // length, *shape[dim + 1 :])
    return jnp.moveaxis(tiles, dim, 0)


def sent_and_summed(array, axis, dim):
    tiles = split_up(array, dim, lax.axis_size(axis))
    arrived = lax.all_to_all(tiles, axis, split_axis=0, concat_axis=0, tiled=True)
    return arrived.sum(axis=0)


def sum_by_axis(array, axes, dim):
    far, near = axes
    tiles = split_up(array, dim, lax.axis_size(far))
    nearer = sent_and_summed(tiles, near, dim + 1)
    arrived = lax.all_to_all(nearer, far, split_axis=0, concat_axis=0, tiled=True)
    return arrived.sum(axis=0)


def rows_for(lines, length):
    spare = -lines.shape[0] % length
    if not spare:
        return lines
    return jnp.concatenate([lines, jnp.zeros((spare, *lines.shape[1:]), lines.dtype)])


def gathered_by_axis(array, axes, dim):
    far, near = axes
    leading = from_everyone(array, far)
    tiles = jnp.swapaxes(from_everyone(leading, near), 0, 1)
    return joined_along(tiles.reshape(-1, *array.shape), dim)


def nested_sum(array, axes):
    lines = array.reshape(-1, array.shape[-1])
    own = sum_by_axis(rows_for(lines, lax.axis_size(axes[0]) * lax.axis_size(axes[1])), axes, 0)
    whole = gathered_by_axis(own, axes, 0)
    return whole[: len(lines)].reshape(array.shape)


def shards(tensor, factor_two, factor_three, factor_four, factor_init):
    highest = lax.Precision.HIGHEST
    first_len = tensor.shape[0]
    local_two = tensor.shape[1]
    fourth_len = factor_four.shape[0]
    local_three = tensor.shape[2] // fourth_len
    rank_one = factor_init.shape[1]
    data = tensor.reshape(first_len, local_two, local_three, fourth_len)
    fourth = jnp.einsum("abcd,de->abce", data, factor_four, precision=highest)
    whole_two = gathered_copies(factor_two, ROW, 0)
    spread_two = lax.all_to_all(fourth, ROW, split_axis=0, concat_axis=1, tiled=True)
    projected_two = jnp.einsum("abce,bg->agce", spread_two, whole_two, precision=highest)
    partial_two = lax.all_to_all(projected_two, ROW, split_axis=1, concat_axis=0, tiled=True)
    whole_three = gathered_copies(factor_three, COL, 0)
    spread_three = lax.all_to_all(partial_two, COL, split_axis=0, concat_axis=2, tiled=True)
    projected_three = jnp.einsum("agce,cf->agfe", spread_three, whole_three, precision=highest)
    block = lax.all_to_all(projected_three, COL, split_axis=2, concat_axis=0, tiled=True)
    columns = block.reshape(first_len, -1)
    basis = factor_init
    inner = jnp.dot(columns.T, basis, precision=highest, preferred_element_type=jnp.float32)
    local_image = jnp.dot(columns, inner, precision=highest, preferred_element_type=jnp.float32)
    image = nested_sum(local_image, (("row_0", "row_1"), ("col_0", "col_1")))
    square = jnp.dot(image.T, image, precision=highest, preferred_element_type=jnp.float32)
    lower = jnp.linalg.cholesky(square)
    basis = jax.scipy.linalg.solve_triangular(lower, image.T, lower=True).T
    core = jnp.dot(basis.T, columns, precision=highest, preferred_element_type=jnp.float32)
    return (basis, core.reshape(rank_one, block.shape[1], block.shape[2], block.shape[3]))


def solution(mesh):
    split = Mesh(mesh.devices.reshape(4, 2, 4, 8), ("row_0", "row_1", "col_0", "col_1"))
    in_specs = (P(None, ROW, COL), P(ROW, None), P(COL, None), P(), P())
    out_specs = (P(), P(None, ROW, COL, None))
    return jax.shard_map(
        shards, mesh=split, in_specs=in_specs, out_specs=out_specs, check_vma=False
    )
```

profile of v0, /device:TPU:32, one launch (start us, length us, event | category | flops | bytes accessed | tf_op | source)
XLA Modules:
  0.0 319.9 jit_solution(13342368360743462871)
XLA Ops:
  6.4 5.4 %copy.77 = f32[1024,8,128]{0,2,1:T(8,128)} copy(f32[1024,8,128]{2,1,0:T(8,128)} %param.5) | data formatting | bytes 8388608 | tf_op args[0]
  16.0 12.2 %copy.78 = f32[1024,8,4,16]{3,2,1,0:T(4,128)} copy(f32[1024,8,4,16]{0,3,2,1:T(8,128)S(1)} %fusion.18) | data formatting | bytes 4194304 | tf_op jit(solution)/shard_map/abcd,de->abce/dot_general | solution.py:76
  28.1 15.4 %reshape.43 = f32[8,1,65536]{2,1,0:T(1,128)} reshape(f32[1024,8,4,16]{3,2,1,0:T(4,128)} %copy.78) | data formatting | bytes 4194304
  43.5 5.3 %all-to-all-start = ((f32[8,1,65536]{2,1,0:T(1,128)}), f32[8,1,65536]{2,1,0:T(1,128)}, u32[]{:S(2)}, u32[]{:S(2)}) async-start(f32[8,1,65536]{2,1,0:T(1,128)} %reshape.43), calls=%async_computation | async-start | bytes 4194304 | tf_op jit(solution)/shard_map/all_to_all | solution.py:78
  50.1 25.5 %all-to-all-done = f32[8,1,65536]{2,1,0:T(1,128)} async-done(((f32[8,1,65536]{2,1,0:T(1,128)}), f32[8,1,65536]{2,1,0:T(1,128)}, u32[]{:S(2)}, u32[]{:S(2)}) %all-to-all-start) | async-done | bytes 2097184 | tf_op jit(solution)/shard_map/all_to_all | solution.py:78
  75.6 7.2 %reduce.6 = f32[8,65536]{1,0:T(8,128)S(1)} reduce(f32[8,1,65536]{2,1,0:T(1,128)} %all-to-all-done, f32[]{:T(128)} %broadcast.53), dimensions={1}, to_apply=%all_to_all.64.reduce_sub_computation | reduce | bytes 4194308 | tf_op jit(solution)/shard_map/all_to_all | solution.py:78
  82.8 17.3 %reshape.44 = f32[1024,8,4,16]{3,2,1,0:T(4,128)} reshape(f32[8,65536]{1,0:T(8,128)S(1)} %reduce.6) | data formatting | bytes 4194304
  100.1 10.0 %copy.106 = f32[8,128,8,4,16]{1,0,3,4,2:T(8,128)S(1)} copy(f32[8,128,8,4,16]{4,3,2,1,0:T(4,128)} %bitcast.89) | data formatting | bytes 4194304 | tf_op jit(solution)/shard_map/all_to_all | solution.py:78
  117.4 15.1 %all-to-all-done.2 = f32[128,32,4,16]{0,3,2,1:T(8,128)S(1)} async-done(((f32[128,32,4,16]{0,3,2,1:T(8,128)}), f32[128,32,4,16]{0,3,2,1:T(8,128)S(1)}, u32[]{:S(2)}, u32[]{:S(2)}) %all-to-all-start.2) | async-done | bytes 1048608 | tf_op jit(solution)/shard_map/all_to_all | solution.py:80
  132.5 11.4 %all-to-all-start.4 = ((f32[32,1,128]{2,1,0:T(1,128)}), f32[32,1,128]{2,1,0:T(1,128)S(1)}, u32[]{:S(2)}, u32[]{:S(2)}) async-start(f32[32,1,128]{2,1,0:T(1,128)} %reshape.49), calls=%async_computation.4 | async-start | bytes 32768 | tf_op jit(solution)/shard_map/all_to_all | solution.py:13
  143.8 6.1 %copy.110 = f32[8,128,4,4,16]{4,3,2,1,0:T(4,128)} copy(f32[8,128,4,4,16]{1,4,3,2,0:T(8,128)S(1)} %bitcast.93) | data formatting | bytes 2097152 | tf_op jit(solution)/shard_map/all_to_all | solution.py:80
  150.0 8.9 %reshape.47 = f32[32,1,8192]{2,1,0:T(1,128)} reshape(f32[1024,4,4,16]{3,2,1,0:T(4,128)} %bitcast.90) | data formatting | bytes 2097152
  158.9 10.1 %all-to-all-start.3 = ((f32[32,1,8192]{2,1,0:T(1,128)}), f32[32,1,8192]{2,1,0:T(1,128)S(1)}, u32[]{:S(2)}, u32[]{:S(2)}) async-start(f32[32,1,8192]{2,1,0:T(1,128)} %reshape.47), calls=%async_computation.3 | async-start | bytes 2097152 | tf_op jit(solution)/shard_map/all_to_all | solution.py:82
  169.8 26.8 %all-to-all-done.3 = f32[32,1,8192]{2,1,0:T(1,128)S(1)} async-done(((f32[32,1,8192]{2,1,0:T(1,128)}), f32[32,1,8192]{2,1,0:T(1,128)S(1)}, u32[]{:S(2)}, u32[]{:S(2)}) %all-to-all-start.3) | async-done | bytes 1048608 | tf_op jit(solution)/shard_map/all_to_all | solution.py:82
  199.8 7.2 %reshape.48 = f32[1024,4,4,16]{3,2,1,0:T(4,128)} reshape(f32[32,8192]{1,0:T(8,128)S(1)} %reduce.8) | data formatting | bytes 2097152
  207.1 10.0 %copy.85 = f32[32,32,4,4,16]{0,1,3,4,2:T(8,128)} copy(f32[32,32,4,4,16]{4,3,2,1,0:T(4,128)} %bitcast.91) | data formatting | bytes 2097152 | tf_op jit(solution)/shard_map/all_to_all | solution.py:82
  217.1 5.6 %fusion.7 = f32[32,4,32,16]{2,0,3,1:T(8,128)S(1)} fusion(f32[32,32,4,4,16]{0,1,3,4,2:T(8,128)} %copy.85, f32[32,4,32,1,1]{2,1,0,4,3:T(4,128)S(1)} %bitcast.99), kind=kOutput, calls=%fused_computation.5 | convolution fusion | flops 100663296 | bytes 1327104 | tf_op jit(solution)/shard_map/agce,cf->agfe/dot_general | solution.py:83
  224.1 16.8 %all_to_all.93 = f32[32,1,2048]{2,1,0:T(1,128)S(1)} all-to-all(f32[32,1,2048]{2,1,0:T(1,128)S(1)} %reshape.51), channel_id=1, replica_groups=mesh['row_0'=4,'row_1'=2,'col_0'=4,'col_1'=8] {'col_0','col_1'}, dimensions={0} | all-to-all | bytes 524288 | tf_op jit(solution)/shard_map/all_to_all | solution.py:84
  249.7 15.8 %all_to_all.94 = f32[32,1,2048]{2,1,0:T(1,128)S(1)} all-to-all(f32[32,1,2048]{2,1,0:T(1,128)S(1)} %reshape.53), channel_id=1, replica_groups=mesh['row_0'=4,'row_1'=2,'col_0'=4,'col_1'=8] {'col_0','col_1'}, dimensions={0} | all-to-all | bytes 524288 | tf_op jit(solution)/shard_map/all_to_all | solution.py:35
  267.3 7.7 %all_to_all.95 = f32[8,1,256]{2,1,0:T(1,128)S(1)} all-to-all(f32[8,1,256]{2,1,0:T(1,128)S(1)} %reshape.55), channel_id=1, replica_groups=mesh['row_0'=4,'row_1'=2,'col_0'=4,'col_1'=8] {'row_0','row_1'}, dimensions={0} | all-to-all | bytes 16384 | tf_op jit(solution)/shard_map/all_to_all | solution.py:43
  275.9 7.7 %all_to_all.96 = f32[8,1,256]{2,1,0:T(1,128)S(1)} all-to-all(f32[8,1,256]{2,1,0:T(1,128)S(1)} %reshape.57), channel_id=1, replica_groups=mesh['row_0'=4,'row_1'=2,'col_0'=4,'col_1'=8] {'row_0','row_1'}, dimensions={0} | all-to-all | bytes 16384 | tf_op jit(solution)/shard_map/all_to_all | solution.py:13
  284.9 16.9 %all_to_all.97 = f32[32,1,2048]{2,1,0:T(1,128)S(1)} all-to-all(f32[32,1,2048]{2,1,0:T(1,128)S(1)} %reshape.59), channel_id=1, replica_groups=mesh['row_0'=4,'row_1'=2,'col_0'=4,'col_1'=8] {'col_0','col_1'}, dimensions={0} | all-to-all | bytes 524288 | tf_op jit(solution)/shard_map/all_to_all | solution.py:13
  305.2 5.8 %cholesky.16 = f32[64,64]{1,0:T(8,128)S(1)} custom-call(f32[64,64]{1,0:T(8,128)S(1)} %fusion.16), custom_call_target="Cholesky" | custom-call | tf_op jit(solution)/shard_map/jit(cholesky)/cholesky | solution.py:91
  312.4 4.9 %custom-call.7 = f32[1,64,64]{1,2,0:T(8,128)S(1)} custom-call(f32[1,64,64]{2,1,0:T(8,128)S(1)} %fusion.13), custom_call_target="InvertDiagBlocksLowerTriangular" | custom-call | tf_op jit(solution)/shard_map/jit(_solve_triangular)/triangular_solve | solution.py:92
  (63 shorter events, 43.3 us)
Async XLA Ops:
  0.6 247.3 %copy-start = (f32[1024,64]{0,1:T(8,128)S(1)}, f32[1024,64]{0,1:T(8,128)}, u32[]{:S(2)}) copy-start(f32[1024,64]{0,1:T(8,128)} %param.9) | copy-start | bytes 786436
  2.1 41.5 %all-to-all-start.1 = ((f32[8,1,256]{2,1,0:T(1,128)}), f32[8,1,256]{2,1,0:T(1,128)S(1)}, u32[]{:S(2)}, u32[]{:S(2)}) async-start(f32[8,1,256]{2,1,0:T(1,128)} %reshape.45), calls=%async_computation.1 | async-start | bytes 16384 | tf_op jit(solution)/shard_map/all_to_all | solution.py:13
  6.4 5.4 %copy-start.2 = (f32[32,16]{0,1:T(8,128)S(1)}, f32[32,16]{0,1:T(8,128)}, u32[]{:S(2)}) copy-start(f32[32,16]{0,1:T(8,128)} %param.8) | copy-start | bytes 6148
  43.5 32.1 %all-to-all-start = ((f32[8,1,65536]{2,1,0:T(1,128)}), f32[8,1,65536]{2,1,0:T(1,128)}, u32[]{:S(2)}, u32[]{:S(2)}) async-start(f32[8,1,65536]{2,1,0:T(1,128)} %reshape.43), calls=%async_computation | async-start | bytes 4194304 | tf_op jit(solution)/shard_map/all_to_all | solution.py:78
  110.1 6.5 %copy-start.3 = (f32[4,32]{1,0:T(4,128)S(1)}, f32[4,32]{1,0:T(4,128)}, u32[]{:S(2)}) copy-start(f32[4,32]{1,0:T(4,128)} %param.7) | copy-start | bytes 1540
  113.1 19.4 %all-to-all-start.2 = ((f32[128,32,4,16]{0,3,2,1:T(8,128)}), f32[128,32,4,16]{0,3,2,1:T(8,128)S(1)}, u32[]{:S(2)}, u32[]{:S(2)}) async-start(f32[128,32,4,16]{0,3,2,1:T(8,128)} %copy.81), calls=%async_computation.2 | async-start | bytes 2097152 | tf_op jit(solution)/shard_map/all_to_all | solution.py:80
  132.5 26.4 %all-to-all-start.4 = ((f32[32,1,128]{2,1,0:T(1,128)}), f32[32,1,128]{2,1,0:T(1,128)S(1)}, u32[]{:S(2)}, u32[]{:S(2)}) async-start(f32[32,1,128]{2,1,0:T(1,128)} %reshape.49), calls=%async_computation.4 | async-start | bytes 32768 | tf_op jit(solution)/shard_map/all_to_all | solution.py:13
  158.9 37.7 %all-to-all-start.3 = ((f32[32,1,8192]{2,1,0:T(1,128)}), f32[32,1,8192]{2,1,0:T(1,128)S(1)}, u32[]{:S(2)}, u32[]{:S(2)}) async-start(f32[32,1,8192]{2,1,0:T(1,128)} %reshape.47), calls=%async_computation.3 | async-start | bytes 2097152 | tf_op jit(solution)/shard_map/all_to_all | solution.py:82
  318.4 1.0 copy-start.1
where the time goes:
time: 325 us; the launch traced here: 320 us
  local copies, waits for them, and re-layouts  107 us (33%)
  waiting for transfers between devices  67.4 us (21%)
  blocking collectives  64.8 us (20%)
  starting transfers between devices  34.6 us (11%)
  other arithmetic  29.1 us (9%)
  matrix products  15.2 us (5%)
    unnamed x27, local copies, waits for them, and re-layouts  58.6 us
    all_to_all x1, waiting for transfers between devices, shards(): lax.all_to_all(partial_two, COL, split_axis=0, concat_axis=2, tiled=True)  26.8 us
    all_to_all x1, waiting for transfers between devices, shards(): lax.all_to_all(fourth, ROW, split_axis=0, concat_axis=1, tiled=True)  25.5 us
    all_to_all x2, blocking collectives, from_everyone(): return lax.all_to_all(copies, axis, split_axis=0, concat_axis=0, tiled=True)  24.5 us
    all_to_all x1, blocking collectives, shards(): lax.all_to_all(projected_three, COL, split_axis=2, concat_axis=0, tiled=T...  16.8 us
    all_to_all x1, blocking collectives, sent_and_summed(): lax.all_to_all(tiles, axis, split_axis=0, concat_axis=0, tiled=True)  15.8 us
    all_to_all x2, starting transfers between devices, from_everyone(): return lax.all_to_all(copies, axis, split_axis=0, concat_axis=0, tiled=True)  15.7 us
    all_to_all x1, waiting for transfers between devices, shards(): lax.all_to_all(projected_two, ROW, split_axis=1, concat_axis=0, tiled=True)  15.1 us
  transfers between devices with their start and end apart: 5, of which 3 were waited for; matrix products, arithmetic and copies ran while one was open for 17% of the time, Pallas kernels for 0%

commit v1 on v0

--- a/solution.py
+++ b/solution.py
@@ -75,7 +75,10 @@
     data = tensor.reshape(first_len, local_two, local_three, fourth_len)
     fourth = jnp.einsum("abcd,de->abce", data, factor_four, precision=highest)
     whole_two = gathered_copies(factor_two, ROW, 0)
-    spread_two = lax.all_to_all(fourth, ROW, split_axis=0, concat_axis=1, tiled=True)
+    spread_two = jnp.concatenate(
+        jax.lax.all_to_all(jnp.stack(jnp.split(fourth, jax.lax.psum(1, ROW), axis=0)), ROW, 0, 0),
+        axis=1,
+    )
     projected_two = jnp.einsum("abce,bg->agce", spread_two, whole_two, precision=highest)
     partial_two = lax.all_to_all(projected_two, ROW, split_axis=1, concat_axis=0, tiled=True)
     whole_three = gathered_copies(factor_three, COL, 0)

time: 325 us -> 260 us (0.80); the launches traced: 320 us -> 259 us
  local copies, waits for them, and re-layouts: 107 us -> 54.1 us
  other arithmetic: 29.1 us -> 21.9 us
    unnamed x27 -> x34, local copies, waits for them, and re-layouts: 58.6 us -> 27.5 us
    dot_general x1 -> x0, local copies, waits for them, and re-layouts: 12.2 us -> none  [shards(): fourth = jnp.einsum('abcd,de->abce', data, factor_four, precision=highest)]
    all_to_all x2 -> x0, local copies, waits for them, and re-layouts: 10.5 us -> none  [shards(): lax.all_to_all(fourth, ROW, split_axis=0, concat_axis=1, tiled=True)]
    all_to_all x1 -> x0, other arithmetic: 7.22 us -> none  [shards(): lax.all_to_all(fourth, ROW, split_axis=0, concat_axis=1, tiled=True)]
  transfers between devices with their start and end apart: 5 -> 5, of which waited for: 3 -> 3; matrix products, arithmetic and copies ran while one was open for 17% -> 11% of each run, Pallas kernels for 0% -> 0%
where the time goes in v1:
time: 260 us; the launch traced here: 259 us
  waiting for transfers between devices  68 us (26%)
  blocking collectives  64.3 us (25%)
  local copies, waits for them, and re-layouts  54.1 us (21%)
  starting transfers between devices  33.8 us (13%)
  other arithmetic  21.9 us (8%)
  matrix products  16.3 us (6%)
    unnamed x34, local copies, waits for them, and re-layouts  27.5 us
    all_to_all x1, waiting for transfers between devices, shards(): lax.all_to_all(partial_two, COL, split_axis=0, concat_axis=2, tiled=True)  26.9 us
    all_to_all x1, waiting for transfers between devices, shards(): jax.lax.all_to_all(jnp.stack(jnp.split(fourth, jax.lax.psum(1, ROW), axis...  25.9 us
    all_to_all x2, blocking collectives, from_everyone(): return lax.all_to_all(copies, axis, split_axis=0, concat_axis=0, tiled=True)  24.3 us
    all_to_all x1, blocking collectives, shards(): lax.all_to_all(projected_three, COL, split_axis=2, concat_axis=0, tiled=T...  16.5 us
    all_to_all x1, blocking collectives, sent_and_summed(): lax.all_to_all(tiles, axis, split_axis=0, concat_axis=0, tiled=True)  15.8 us
    all_to_all x2, starting transfers between devices, from_everyone(): return lax.all_to_all(copies, axis, split_axis=0, concat_axis=0, tiled=True)  15.7 us
    all_to_all x1, waiting for transfers between devices, shards(): lax.all_to_all(projected_two, ROW, split_axis=1, concat_axis=0, tiled=True)  15.1 us
  transfers between devices with their start and end apart: 5, of which 3 were waited for; matrix products, arithmetic and copies ran while one was open for 11% of the time, Pallas kernels for 0%

profile of v1, /device:TPU:32, one launch (start us, length us, event | category | flops | bytes accessed | tf_op | source)
XLA Modules:
  0.0 259.4 jit_solution(12607006318543335760)
XLA Ops:
  2.1 4.3 %all-to-all-start.1 = ((f32[8,1,256]{2,1,0:T(1,128)}), f32[8,1,256]{2,1,0:T(1,128)S(1)}, u32[]{:S(2)}, u32[]{:S(2)}) async-start(f32[8,1,256]{2,1,0:T(1,128)} %reshape.48), calls=%async_computation.1 | async-start | bytes 16384 | tf_op jit(solution)/shard_map/all_to_all | solution.py:13
  6.4 5.4 %copy.55 = f32[1024,8,128]{0,2,1:T(8,128)} copy(f32[1024,8,128]{2,1,0:T(8,128)} %param.5) | data formatting | bytes 8388608 | tf_op args[0]
  11.8 4.2 %fusion.26 = f32[1024,8,4,16]{0,3,2,1:T(8,128)S(1)} fusion(f32[1024,8,4,32]{0,3,2,1:T(8,128)} %bitcast.122, f32[32,16]{0,1:T(8,128)S(1)} %copy-done.3), kind=kOutput, calls=%fused_computation.40 | convolution fusion | flops 201326592 | bytes 6293504 | tf_op jit(solution)/shard_map/abcd,de->abce/dot_general | solution.py:76
  17.7 4.8 %all-to-all-start = ((f32[8,128,8,4,16]{1,4,3,2,0:T(8,128)}), f32[8,128,8,4,16]{1,4,3,2,0:T(8,128)S(1)}, u32[]{:S(2)}, u32[]{:S(2)}) async-start(f32[8,128,8,4,16]{1,4,3,2,0:T(8,128)} %copy-done.1), calls=%async_computation | async-start | bytes 4194304 | tf_op jit(solution)/shard_map/all_to_all | solution.py:79
  23.7 25.9 %all-to-all-done = f32[8,128,8,4,16]{1,4,3,2,0:T(8,128)S(1)} async-done(((f32[8,128,8,4,16]{1,4,3,2,0:T(8,128)}), f32[8,128,8,4,16]{1,4,3,2,0:T(8,128)S(1)}, u32[]{:S(2)}, u32[]{:S(2)}) %all-to-all-start) | async-done | bytes 2097184 | tf_op jit(solution)/shard_map/all_to_all | solution.py:79
  49.6 2.5 fusion.4
  53.7 3.6 %all-to-all-start.2 = ((f32[128,32,4,16]{0,3,2,1:T(8,128)}), f32[128,32,4,16]{0,3,2,1:T(8,128)S(1)}, u32[]{:S(2)}, u32[]{:S(2)}) async-start(f32[128,32,4,16]{0,3,2,1:T(8,128)} %copy.57), calls=%async_computation.2 | async-start | bytes 2097152 | tf_op jit(solution)/shard_map/all_to_all | solution.py:83
  58.0 15.1 %all-to-all-done.2 = f32[128,32,4,16]{0,3,2,1:T(8,128)S(1)} async-done(((f32[128,32,4,16]{0,3,2,1:T(8,128)}), f32[128,32,4,16]{0,3,2,1:T(8,128)S(1)}, u32[]{:S(2)}, u32[]{:S(2)}) %all-to-all-start.2) | async-done | bytes 1048608 | tf_op jit(solution)/shard_map/all_to_all | solution.py:83
  73.2 11.4 %all-to-all-start.4 = ((f32[32,1,128]{2,1,0:T(1,128)}), f32[32,1,128]{2,1,0:T(1,128)S(1)}, u32[]{:S(2)}, u32[]{:S(2)}) async-start(f32[32,1,128]{2,1,0:T(1,128)} %reshape.52), calls=%async_computation.4 | async-start | bytes 32768 | tf_op jit(solution)/shard_map/all_to_all | solution.py:13
  84.5 6.1 %copy.80 = f32[8,128,4,4,16]{4,3,2,1,0:T(4,128)} copy(f32[8,128,4,4,16]{1,4,3,2,0:T(8,128)S(1)} %bitcast.124) | data formatting | bytes 2097152 | tf_op jit(solution)/shard_map/all_to_all | solution.py:83
  90.6 8.9 %reshape.50 = f32[32,1,8192]{2,1,0:T(1,128)} reshape(f32[1024,4,4,16]{3,2,1,0:T(4,128)} %bitcast.120) | data formatting | bytes 2097152
  99.6 9.8 %all-to-all-start.3 = ((f32[32,1,8192]{2,1,0:T(1,128)}), f32[32,1,8192]{2,1,0:T(1,128)S(1)}, u32[]{:S(2)}, u32[]{:S(2)}) async-start(f32[32,1,8192]{2,1,0:T(1,128)} %reshape.50), calls=%async_computation.3 | async-start | bytes 2097152 | tf_op jit(solution)/shard_map/all_to_all | solution.py:85
  110.2 26.9 %all-to-all-done.3 = f32[32,1,8192]{2,1,0:T(1,128)S(1)} async-done(((f32[32,1,8192]{2,1,0:T(1,128)}), f32[32,1,8192]{2,1,0:T(1,128)S(1)}, u32[]{:S(2)}, u32[]{:S(2)}) %all-to-all-start.3) | async-done | bytes 1048608 | tf_op jit(solution)/shard_map/all_to_all | solution.py:85
  137.1 3.2 %reduce.7 = f32[32,8192]{1,0:T(8,128)S(1)} reduce(f32[32,1,8192]{2,1,0:T(1,128)S(1)} %all-to-all-done.3, f32[]{:T(128)} %broadcast.53), dimensions={1}, to_apply=%all_to_all.62.reduce_sub_computation | reduce | bytes 2097156 | tf_op jit(solution)/shard_map/all_to_all | solution.py:85
  140.3 7.2 %reshape.51 = f32[1024,4,4,16]{3,2,1,0:T(4,128)} reshape(f32[32,8192]{1,0:T(8,128)S(1)} %reduce.7) | data formatting | bytes 2097152
  147.6 10.0 %copy.61 = f32[32,32,4,4,16]{0,1,3,4,2:T(8,128)} copy(f32[32,32,4,4,16]{4,3,2,1,0:T(4,128)} %bitcast.121) | data formatting | bytes 2097152 | tf_op jit(solution)/shard_map/all_to_all | solution.py:85
  157.6 5.6 %fusion.7 = f32[32,4,32,16]{2,0,3,1:T(8,128)S(1)} fusion(f32[32,32,4,4,16]{0,1,3,4,2:T(8,128)} %copy.61, f32[32,4,32,1,1]{2,1,0,4,3:T(4,128)S(1)} %bitcast.130), kind=kOutput, calls=%fused_computation.5 | convolution fusion | flops 100663296 | bytes 1327104 | tf_op jit(solution)/shard_map/agce,cf->agfe/dot_general | solution.py:86
  164.6 16.5 %all_to_all.83 = f32[32,1,2048]{2,1,0:T(1,128)S(1)} all-to-all(f32[32,1,2048]{2,1,0:T(1,128)S(1)} %reshape.54), channel_id=1, replica_groups=mesh['row_0'=4,'row_1'=2,'col_0'=4,'col_1'=8] {'col_0','col_1'}, dimensions={0} | all-to-all | bytes 524288 | tf_op jit(solution)/shard_map/all_to_all | solution.py:87
  189.9 15.8 %all_to_all.84 = f32[32,1,2048]{2,1,0:T(1,128)S(1)} all-to-all(f32[32,1,2048]{2,1,0:T(1,128)S(1)} %reshape.56), channel_id=1, replica_groups=mesh['row_0'=4,'row_1'=2,'col_0'=4,'col_1'=8] {'col_0','col_1'}, dimensions={0} | all-to-all | bytes 524288 | tf_op jit(solution)/shard_map/all_to_all | solution.py:35
  207.6 7.7 %all_to_all.85 = f32[8,1,256]{2,1,0:T(1,128)S(1)} all-to-all(f32[8,1,256]{2,1,0:T(1,128)S(1)} %reshape.58), channel_id=1, replica_groups=mesh['row_0'=4,'row_1'=2,'col_0'=4,'col_1'=8] {'row_0','row_1'}, dimensions={0} | all-to-all | bytes 16384 | tf_op jit(solution)/shard_map/all_to_all | solution.py:43
  216.1 7.7 %all_to_all.86 = f32[8,1,256]{2,1,0:T(1,128)S(1)} all-to-all(f32[8,1,256]{2,1,0:T(1,128)S(1)} %reshape.60), channel_id=1, replica_groups=mesh['row_0'=4,'row_1'=2,'col_0'=4,'col_1'=8] {'row_0','row_1'}, dimensions={0} | all-to-all | bytes 16384 | tf_op jit(solution)/shard_map/all_to_all | solution.py:13
  225.1 16.6 %all_to_all.87 = f32[32,1,2048]{2,1,0:T(1,128)S(1)} all-to-all(f32[32,1,2048]{2,1,0:T(1,128)S(1)} %reshape.62), channel_id=1, replica_groups=mesh['row_0'=4,'row_1'=2,'col_0'=4,'col_1'=8] {'col_0','col_1'}, dimensions={0} | all-to-all | bytes 524288 | tf_op jit(solution)/shard_map/all_to_all | solution.py:13
  245.2 5.8 %cholesky.16 = f32[64,64]{1,0:T(8,128)S(1)} custom-call(f32[64,64]{1,0:T(8,128)S(1)} %fusion.25), custom_call_target="Cholesky" | custom-call | tf_op jit(solution)/shard_map/jit(cholesky)/cholesky | solution.py:94
  252.4 4.9 %custom-call.7 = f32[1,64,64]{1,2,0:T(8,128)S(1)} custom-call(f32[1,64,64]{2,1,0:T(8,128)S(1)} %fusion.21), custom_call_target="InvertDiagBlocksLowerTriangular" | custom-call | tf_op jit(solution)/shard_map/jit(_solve_triangular)/triangular_solve | solution.py:95
  (68 shorter events, 28.3 us)
Async XLA Ops:
  0.6 187.5 %copy-start = (f32[1024,64]{0,1:T(8,128)S(1)}, f32[1024,64]{0,1:T(8,128)}, u32[]{:S(2)}) copy-start(f32[1024,64]{0,1:T(8,128)} %param.9) | copy-start | bytes 786436
  2.1 15.6 %all-to-all-start.1 = ((f32[8,1,256]{2,1,0:T(1,128)}), f32[8,1,256]{2,1,0:T(1,128)S(1)}, u32[]{:S(2)}, u32[]{:S(2)}) async-start(f32[8,1,256]{2,1,0:T(1,128)} %reshape.48), calls=%async_computation.1 | async-start | bytes 16384 | tf_op jit(solution)/shard_map/all_to_all | solution.py:13
  6.4 5.4 %copy-start.3 = (f32[32,16]{0,1:T(8,128)S(1)}, f32[32,16]{0,1:T(8,128)}, u32[]{:S(2)}) copy-start(f32[32,16]{0,1:T(8,128)} %param.8) | copy-start | bytes 6148
  16.3 1.4 copy-start.1
  17.7 32.0 %all-to-all-start = ((f32[8,128,8,4,16]{1,4,3,2,0:T(8,128)}), f32[8,128,8,4,16]{1,4,3,2,0:T(8,128)S(1)}, u32[]{:S(2)}, u32[]{:S(2)}) async-start(f32[8,128,8,4,16]{1,4,3,2,0:T(8,128)} %copy-done.1), calls=%async_computation | async-start | bytes 4194304 | tf_op jit(solution)/shard_map/all_to_all | solution.py:79
  52.1 5.2 %copy-start.4 = (f32[4,32]{1,0:T(4,128)S(1)}, f32[4,32]{1,0:T(4,128)}, u32[]{:S(2)}) copy-start(f32[4,32]{1,0:T(4,128)} %param.7) | copy-start | bytes 1540
  53.7 19.4 %all-to-all-start.2 = ((f32[128,32,4,16]{0,3,2,1:T(8,128)}), f32[128,32,4,16]{0,3,2,1:T(8,128)S(1)}, u32[]{:S(2)}, u32[]{:S(2)}) async-start(f32[128,32,4,16]{0,3,2,1:T(8,128)} %copy.57), calls=%async_computation.2 | async-start | bytes 2097152 | tf_op jit(solution)/shard_map/all_to_all | solution.py:83
  73.2 26.4 %all-to-all-start.4 = ((f32[32,1,128]{2,1,0:T(1,128)}), f32[32,1,128]{2,1,0:T(1,128)S(1)}, u32[]{:S(2)}, u32[]{:S(2)}) async-start(f32[32,1,128]{2,1,0:T(1,128)} %reshape.52), calls=%async_computation.4 | async-start | bytes 32768 | tf_op jit(solution)/shard_map/all_to_all | solution.py:13
  99.6 37.5 %all-to-all-start.3 = ((f32[32,1,8192]{2,1,0:T(1,128)}), f32[32,1,8192]{2,1,0:T(1,128)S(1)}, u32[]{:S(2)}, u32[]{:S(2)}) async-start(f32[32,1,8192]{2,1,0:T(1,128)} %reshape.50), calls=%async_computation.3 | async-start | bytes 2097152 | tf_op jit(solution)/shard_map/all_to_all | solution.py:85
  258.4 1.0 copy-start.2
